TPU v7x, 32 devices: a whole 2x2x4 slice. The times are simulated.
32 devices in a mesh: ep: 4 (over y, x), grp: 8 (over z, core).
Axes of the slice: x: 2, y: 2, z: 4, core: 2. Of those that a mesh axis runs over, the one named last changes fastest.
Arguments:
- tokens: bfloat16 [4096, 4096], P(('ep', 'grp')), may hold values from -6 to 6
- expert_ids: int32 [4096, 8], P(('ep', 'grp')), may hold values from 0 to 127, all different within a row; in each aligned block of 128 rows (0 to 127, 128 to 255, ...) at most 16 rows name the same one
- combine: float32 [4096, 8], P(('ep', 'grp')), may hold values from 0.05 to 1
- w_gate: bfloat16 [4096, 1280], P(None, 'ep'), may hold values from -0.09375 to 0.09375
- w_up: bfloat16 [4096, 1280], P(None, 'ep'), may hold values from -0.09375 to 0.09375
- w_down: bfloat16 [1280, 4096], P('ep'), may hold values from -0.15625 to 0.15625
- bias: float32 [128], replicated, may hold values from -3 to 3
Outputs:
- mixed: bfloat16 [4096, 4096], P(('ep', 'grp'))
- new_bias: float32 [128], replicated
Inputs may be any that keep to these rules, and one draw needn't show every extreme that they name: `expert_ids`: each row names 8 different experts. Among the rows of one device no expert is named more than 16 times, a bound that some block reaches.
All inputs are finite; a program needn't handle non-finite values.
Results may differ from a plain program's by a relative error of at most 0.0057.
Values may be sent and summed in bfloat16 or wider, within the bound.
A program may use at most 64 MiB of HBM per device.

v0:
```python
import jax
import jax.numpy as jnp
from jax import lax
from jax.sharding import PartitionSpec as P

NEXP = 128
TOPK = 8
SPLIT = 4


def count_loads(expert_ids):
    experts = jnp.arange(NEXP, dtype=jnp.int32)
    local = jnp.sum(
        (expert_ids.reshape(-1)[:, None] == experts[None, :]).astype(jnp.float32), axis=0
    )
    within = lax.psum(local, "ep")
    return lax.psum(within, "grp")


def per_device(tokens, expert_ids, combine, w_gate, w_up, w_down, bias):
    n_ep = lax.axis_size("ep")
    n_grp = lax.axis_size("grp")
    tok_rows = tokens.shape[0]
    width = tokens.shape[1]
    capacity = tok_rows // 8
    win_experts = n_ep // SPLIT
    flat_ids = expert_ids.reshape(-1)
    window = jnp.arange(win_experts, dtype=jnp.int32)
    hit = (flat_ids[:, None] == window[None, :]).astype(jnp.int32)
    ranks = jnp.cumsum(hit, axis=0) - 1
    slot = jnp.sum(hit * ranks, axis=1)
    inside = jnp.sum(hit, axis=1)
    dest = jnp.where(inside > 0, flat_ids * capacity + slot, win_experts * capacity)
    slot_ids = jnp.arange(win_experts * capacity, dtype=jnp.int32)
    chosen = (slot_ids[:, None] == dest[None, :]).reshape(win_experts * capacity, tok_rows, TOPK)
    select = jnp.sum(chosen.astype(jnp.float32), axis=2)
    weights = jnp.sum(chosen.astype(jnp.float32) * combine[None, :, :], axis=2)
    buffer = jnp.dot(
        select.astype(jnp.bfloat16), tokens, preferred_element_type=jnp.float32
    ).astype(jnp.bfloat16)
    outgoing = jnp.repeat(buffer.reshape(win_experts, capacity, width), SPLIT, axis=0)
    block = lax.all_to_all(outgoing, "ep", split_axis=0, concat_axis=0, tiled=True)
    rows = block.reshape(-1, width)
    gate = jnp.dot(rows, w_gate, preferred_element_type=jnp.float32)
    upval = jnp.dot(rows, w_up, preferred_element_type=jnp.float32)
    hidden = (jax.nn.silu(gate) * upval).astype(jnp.bfloat16)
    part = jnp.dot(hidden, w_down, preferred_element_type=jnp.float32).astype(jnp.bfloat16)
    returned = lax.all_to_all(
        part.reshape(block.shape), "ep", split_axis=0, concat_axis=0, tiled=True
    )
    summed = jnp.sum(
        returned.astype(jnp.float32).reshape(win_experts, SPLIT, capacity, width), axis=1
    )
    summed = summed.reshape(win_experts * capacity, width)
    mixed = jnp.dot(
        weights.T, summed, precision=lax.Precision.HIGHEST, preferred_element_type=jnp.float32
    ).astype(jnp.bfloat16)
    load = count_loads(expert_ids)
    mean_load = jnp.float32(tok_rows * n_ep * n_grp * TOPK / NEXP)
    new_bias = bias - 0.05 * (load - mean_load) / jnp.sqrt(mean_load)
    return (mixed, new_bias)


def solution(mesh):
    return jax.shard_map(
        per_device,
        mesh=mesh,
        in_specs=(
            P(("ep", "grp"), None),
            P(("ep", "grp"), None),
            P(("ep", "grp"), None),
            P(None, "ep"),
            P(None, "ep"),
            P("ep", None),
            P(),
        ),
        out_specs=(P(("ep", "grp"), None), P()),
        check_vma=False,
    )
```

profile of v0, /device:TPU:0, one launch (start us, length us, event | category | flops | bytes accessed | tf_op | source)
XLA Modules:
  0.0 56.3 jit_solution(11772067957491407302)
XLA Ops:
  0.6 0.0 copy-start
  0.6 0.8 %fusion.8 = s32[128,8]{0,1:T(8,128)S(1)} fusion(s32[128,8]{0,1:T(8,128)} %param.8), kind=kLoop, calls=%fused_computation.21 | loop fusion | flops 2048 | bytes 8192 | tf_op jit(solution)/shard_map/convert_element_type | solution.py:29
  1.5 0.1 copy.30
  1.6 0.1 reshape.124
  1.7 0.3 reduce-window.6
  2.0 0.2 slice_reduce_fusion
  2.2 0.1 reshape.117
  2.2 0.2 reduce-window.9
  2.4 0.1 broadcast.76
  2.5 0.1 reshape.120
  2.6 0.1 copy.31
  2.7 0.0 copy-start.1
  2.7 0.9 %add_select_fusion = s32[128,8]{0,1:T(8,128)S(1)} fusion(s32[128,8]{0,1:T(8,128)S(1)} %copy.31, s32[128,8]{0,1:T(8,128)S(1)} %copy.32, s32[128,8]{0,1:T(8,128)} %param.8), kind=kLoop, calls=%fused_computation.18 | loop fusion | flops 9216 | bytes 16384 | tf_op jit(solution)/shard_map/jit(_where)/select_n | solution.py:33
  3.6 0.7 %convert_reduce_fusion.2 = (bf16[16,128]{1,0:T(8,128)(2,1)S(1)}, f32[16,128]{1,0:T(8,128)S(1)}) fusion(s32[128,8]{0,1:T(8,128)S(1)} %add_select_fusion, f32[128,8]{0,1:T(8,128)} %param.9), kind=kLoop, calls=%fused_computation.13 | loop fusion | flops 77824 | bytes 20480 | tf_op jit(solution)/shard_map/reduce_sum | solution.py:36
  4.3 1.5 %convolution_convert_fusion.2 = bf16[16,4096]{1,0:T(8,128)(2,1)S(1)} fusion(bf16[128,4096]{1,0:T(8,128)(2,1)} %param.7, bf16[16,128]{1,0:T(8,128)(2,1)S(1)} %get-tuple-element.2), kind=kOutput, calls=%fused_computation.2 | convolution fusion | flops 16842752 | bytes 1183744 | tf_op jit(solution)/shard_map/dot_general | solution.py:38
  5.8 13.5 %all_to_all.10 = bf16[4,16,4096]{2,1,0:T(8,128)(2,1)S(1)} all-to-all(bf16[4,16,4096]{2,1,0:T(8,128)(2,1)S(1)} %reshape.121), channel_id=1, replica_groups=mesh['ep'=4,'grp'=8] {'ep'}, dimensions={0} | all-to-all | bytes 1048576 | tf_op jit(solution)/shard_map/all_to_all | solution.py:42
  19.3 0.0 copy-done.1
  19.3 0.9 %fusion.10 = f32[64,320]{1,0:T(8,128)S(1)} fusion(bf16[64,4096]{1,0:T(8,128)(2,1)S(1)} %bitcast.16, bf16[4096,320]{0,1:T(8,128)(2,1)S(1)} %copy-done.1), kind=kOutput, calls=%fused_computation.25 | convolution fusion | flops 167772160 | bytes 3227648 | tf_op jit(solution)/shard_map/dot_general | solution.py:44
  20.2 0.0 copy-done
  20.2 0.0 copy-start.2
  20.3 0.0 copy-start.3
  20.3 4.7 %convolution_convert_fusion.1 = bf16[64,4096]{1,0:T(8,128)(2,1)} fusion(bf16[320,4096]{1,0:T(8,128)(2,1)S(1)} %copy-done, bf16[64,4096]{1,0:T(8,128)(2,1)S(1)} %bitcast.17, bf16[4096,320]{0,1:T(8,128)(2,1)} %param.11, f32[64,320]{1,0:T(8,128)S(1)} %fusion.10), kind=kOutput, calls=%fused_computation.1 | convolution fusion | flops 335929344 | bytes 6373376 | tf_op jit(solution)/shard_map/dot_general | solution.py:47
  25.0 3.5 %all-to-all-start.1 = ((bf16[4,16,4096]{2,1,0:T(8,128)(2,1)}), bf16[4,16,4096]{2,1,0:T(8,128)(2,1)S(1)}, u32[]{:S(2)}, u32[]{:S(2)}) async-start(bf16[4,16,4096]{2,1,0:T(8,128)(2,1)} %bitcast.18), calls=%async_computation.1 | async-start | bytes 1048576 | tf_op jit(solution)/shard_map/all_to_all | solution.py:48
  28.5 0.0 copy-done.2
  28.5 0.1 copy.33
  28.6 0.1 eq.58
  28.7 0.2 convert_reduce_fusion.1
  28.9 10.4 %psum.14 = f32[128]{0:T(128)S(1)} all-reduce(f32[128]{0:T(128)S(1)} %convert_reduce_fusion.1), channel_id=1, replica_groups=mesh['ep'=4,'grp'=8] {'ep'}, use_global_device_ids=true, to_apply=%region_6.7 | all-reduce | flops 128 | bytes 1024 | tf_op jit(solution)/shard_map/psum | solution.py:16
  39.3 13.6 %psum.15 = f32[128]{0:T(128)S(1)} all-reduce(f32[128]{0:T(128)S(1)} %psum.14), channel_id=1, replica_groups=mesh['ep'=4,'grp'=8] {'grp'}, use_global_device_ids=true, to_apply=%region_7.8 | all-reduce | flops 128 | bytes 1024 | tf_op jit(solution)/shard_map/psum | solution.py:17
  52.9 0.0 copy-done.3
  52.9 0.5 multiply_subtract_fusion
  53.4 0.0 all-to-all-done.1
  53.4 0.1 convert_reduce_fusion
  53.5 2.8 %convolution_convert_fusion = bf16[128,4096]{1,0:T(8,128)(2,1)} fusion(f32[16,128]{1,0:T(8,128)S(1)} %get-tuple-element.3, f32[16,4096]{1,0:T(8,128)S(1)} %convert_reduce_fusion), kind=kOutput, calls=%fused_computation | convolution fusion | flops 101187584 | bytes 1318912 | tf_op jit(solution)/shard_map/dot_general | solution.py:55
  (3 shorter events, 0.1 us)
Async XLA Ops:
  0.6 19.6 %copy-start = (bf16[320,4096]{1,0:T(8,128)(2,1)S(1)}, bf16[320,4096]{1,0:T(8,128)(2,1)}, u32[]{:S(2)}) copy-start(bf16[320,4096]{1,0:T(8,128)(2,1)} %param.12) | copy-start | bytes 7864324
  2.7 16.6 %copy-start.1 = (bf16[4096,320]{0,1:T(8,128)(2,1)S(1)}, bf16[4096,320]{0,1:T(8,128)(2,1)}, u32[]{:S(2)}) copy-start(bf16[4096,320]{0,1:T(8,128)(2,1)} %param.10) | copy-start | bytes 7864324
  20.2 8.2 %copy-start.2 = (s32[128,8]{0,1:T(8,128)S(1)}, s32[128,8]{0,1:T(8,128)}, u32[]{:S(2)}) copy-start(s32[128,8]{0,1:T(8,128)} %param.8) | copy-start | bytes 12292
  20.3 32.6 %copy-start.3 = (f32[128]{0:T(128)S(1)}, f32[128]{0:T(128)}, u32[]{:S(2)}) copy-start(f32[128]{0:T(128)} %param.13) | copy-start | bytes 1540
  25.0 28.4 %all-to-all-start.1 = ((bf16[4,16,4096]{2,1,0:T(8,128)(2,1)}), bf16[4,16,4096]{2,1,0:T(8,128)(2,1)S(1)}, u32[]{:S(2)}, u32[]{:S(2)}) async-start(bf16[4,16,4096]{2,1,0:T(8,128)(2,1)} %bitcast.18), calls=%async_computation.1 | async-start | bytes 1048576 | tf_op jit(solution)/shard_map/all_to_all | solution.py:48
where the time goes:
time: 56.6 us; the launch traced here: 56.3 us
  blocking collectives  37.5 us (66%)
  matrix products  9.9 us (17%)
  other arithmetic  3.71 us (7%)
  starting transfers between devices  3.47 us (6%)
  local copies, waits for them, and re-layouts  1 us (2%)
  between operations  0.72 us (1%)
    psum x1, blocking collectives, count_loads(): return lax.psum(within, 'grp')  13.6 us
    all_to_all x1, blocking collectives, per_device(): lax.all_to_all(outgoing, 'ep', split_axis=0, concat_axis=0, tiled=True)  13.5 us
    psum x1, blocking collectives, count_loads(): within = lax.psum(local, 'ep')  10.4 us
    dot_general x1, matrix products, per_device(): jnp.dot(hidden, w_down, preferred_element_type=jnp.float32)  4.74 us
    all_to_all x1, starting transfers between devices, per_device(): lax.all_to_all(part.reshape(block.shape), 'ep', split_axis=0, concat_axis...  3.47 us
    dot_general x1, matrix products, per_device(): jnp.dot(weights.T, summed, precision=lax.Precision.HIGHEST, preferred_ele...  2.81 us
    dot_general x1, matrix products, per_device(): jnp.dot(select.astype(jnp.bfloat16), tokens, preferred_element_type=jnp.f...  1.47 us
  transfers between devices with their start and end apart: 1, of which 0 were waited for; matrix products, arithmetic and copies ran while one was open for 2% of the time, Pallas kernels for 0%

commit v1 on v0

--- a/solution.py
+++ b/solution.py
@@ -13,7 +13,7 @@
     local = jnp.sum(
         (expert_ids.reshape(-1)[:, None] == experts[None, :]).astype(jnp.float32), axis=0
     )
-    within = lax.psum(local, "ep")
+    within = jnp.sum(lax.all_gather(local, "ep"), axis=0)
     return lax.psum(within, "grp")
 
 

time: 56.6 us -> 54.9 us (0.970)
  blocking collectives: 37.5 us -> 35.7 us
    psum x1 -> x0, blocking collectives: 10.4 us -> none  [count_loads(): within = lax.psum(local, 'ep')]
    all_gather x0 -> x1, blocking collectives: none -> 8.46 us  [count_loads(): within = jnp.sum(lax.all_gather(local, 'ep'), axis=0)]
where the time goes in v1:
time: 54.9 us; the launch traced here: 54.6 us
  blocking collectives  35.7 us (65%)
  matrix products  9.9 us (18%)
  other arithmetic  3.73 us (7%)
  starting transfers between devices  3.47 us (6%)
  local copies, waits for them, and re-layouts  1 us (2%)
  between operations  0.73 us (1%)
    psum x1, blocking collectives, count_loads(): return lax.psum(within, 'grp')  13.8 us
    all_to_all x1, blocking collectives, per_device(): lax.all_to_all(outgoing, 'ep', split_axis=0, concat_axis=0, tiled=True)  13.5 us
    all_gather x1, blocking collectives, count_loads(): within = jnp.sum(lax.all_gather(local, 'ep'), axis=0)  8.46 us
    dot_general x1, matrix products, per_device(): jnp.dot(hidden, w_down, preferred_element_type=jnp.float32)  4.74 us
    all_to_all x1, starting transfers between devices, per_device(): lax.all_to_all(part.reshape(block.shape), 'ep', split_axis=0, concat_axis...  3.47 us
    dot_general x1, matrix products, per_device(): jnp.dot(weights.T, summed, precision=lax.Precision.HIGHEST, preferred_ele...  2.81 us
    dot_general x1, matrix products, per_device(): jnp.dot(select.astype(jnp.bfloat16), tokens, preferred_element_type=jnp.f...  1.47 us
  transfers between devices with their start and end apart: 1, of which 0 were waited for; matrix products, arithmetic and copies ran while one was open for 2% of the time, Pallas kernels for 0%

profile of v1, /device:TPU:0, one launch (start us, length us, event | category | flops | bytes accessed | tf_op | source)
XLA Modules:
  0.0 54.6 jit_solution(14192899444050284648)
XLA Ops:
  0.6 0.0 copy-start
  0.6 0.8 %fusion.8 = s32[128,8]{0,1:T(8,128)S(1)} fusion(s32[128,8]{0,1:T(8,128)} %param.8), kind=kLoop, calls=%fused_computation.21 | loop fusion | flops 2048 | bytes 8192 | tf_op jit(solution)/shard_map/convert_element_type | solution.py:29
  1.5 0.1 copy.40
  1.6 0.1 reshape.124
  1.7 0.3 reduce-window.6
  2.0 0.2 slice_reduce_fusion
  2.2 0.1 reshape.117
  2.2 0.2 reduce-window.9
  2.4 0.1 broadcast.76
  2.5 0.1 reshape.120
  2.6 0.1 copy.41
  2.7 0.0 copy-start.1
  2.7 0.9 %add_select_fusion = s32[128,8]{0,1:T(8,128)S(1)} fusion(s32[128,8]{0,1:T(8,128)S(1)} %copy.41, s32[128,8]{0,1:T(8,128)S(1)} %copy.42, s32[128,8]{0,1:T(8,128)} %param.8), kind=kLoop, calls=%fused_computation.18 | loop fusion | flops 9216 | bytes 16384 | tf_op jit(solution)/shard_map/jit(_where)/select_n | solution.py:33
  3.6 0.7 %convert_reduce_fusion.2 = (bf16[16,128]{1,0:T(8,128)(2,1)S(1)}, f32[16,128]{1,0:T(8,128)S(1)}) fusion(s32[128,8]{0,1:T(8,128)S(1)} %add_select_fusion, f32[128,8]{0,1:T(8,128)} %param.9), kind=kLoop, calls=%fused_computation.13 | loop fusion | flops 77824 | bytes 20480 | tf_op jit(solution)/shard_map/reduce_sum | solution.py:36
  4.3 1.5 %convolution_convert_fusion.2 = bf16[16,4096]{1,0:T(8,128)(2,1)S(1)} fusion(bf16[128,4096]{1,0:T(8,128)(2,1)} %param.7, bf16[16,128]{1,0:T(8,128)(2,1)S(1)} %get-tuple-element.2), kind=kOutput, calls=%fused_computation.2 | convolution fusion | flops 16842752 | bytes 1183744 | tf_op jit(solution)/shard_map/dot_general | solution.py:38
  5.8 13.5 %all_to_all.10 = bf16[4,16,4096]{2,1,0:T(8,128)(2,1)S(1)} all-to-all(bf16[4,16,4096]{2,1,0:T(8,128)(2,1)S(1)} %reshape.121), channel_id=1, replica_groups=mesh['ep'=4,'grp'=8] {'ep'}, dimensions={0} | all-to-all | bytes 1048576 | tf_op jit(solution)/shard_map/all_to_all | solution.py:42
  19.3 0.0 copy-done.1
  19.3 0.9 %fusion.10 = f32[64,320]{1,0:T(8,128)S(1)} fusion(bf16[64,4096]{1,0:T(8,128)(2,1)S(1)} %bitcast.17, bf16[4096,320]{0,1:T(8,128)(2,1)S(1)} %copy-done.1), kind=kOutput, calls=%fused_computation.25 | convolution fusion | flops 167772160 | bytes 3227648 | tf_op jit(solution)/shard_map/dot_general | solution.py:44
  20.2 0.0 copy-done
  20.2 0.0 copy-start.2
  20.3 0.0 copy-start.3
  20.3 4.7 %convolution_convert_fusion.1 = bf16[64,4096]{1,0:T(8,128)(2,1)} fusion(bf16[320,4096]{1,0:T(8,128)(2,1)S(1)} %copy-done, bf16[64,4096]{1,0:T(8,128)(2,1)S(1)} %bitcast.18, bf16[4096,320]{0,1:T(8,128)(2,1)} %param.11, f32[64,320]{1,0:T(8,128)S(1)} %fusion.10), kind=kOutput, calls=%fused_computation.1 | convolution fusion | flops 335929344 | bytes 6373376 | tf_op jit(solution)/shard_map/dot_general | solution.py:47
  25.0 3.5 %all-to-all-start.1 = ((bf16[4,16,4096]{2,1,0:T(8,128)(2,1)}), bf16[4,16,4096]{2,1,0:T(8,128)(2,1)S(1)}, u32[]{:S(2)}, u32[]{:S(2)}) async-start(bf16[4,16,4096]{2,1,0:T(8,128)(2,1)} %bitcast.19), calls=%async_computation.1 | async-start | bytes 1048576 | tf_op jit(solution)/shard_map/all_to_all | solution.py:48
  28.5 0.0 copy-done.2
  28.5 0.1 copy.43
  28.6 0.1 eq.58
  28.7 0.2 convert_reduce_fusion.1
  28.9 8.5 %all-gather.1 = f32[4,1,128]{2,1,0:T(1,128)S(1)} all-gather(f32[1,1,128]{2,1,0:T(1,128)S(1)} %bitcast.20), channel_id=2, replica_groups=mesh['ep'=4,'grp'=8] {'ep'}, dimensions={0}, use_global_device_ids=true | all-gather | bytes 2560 | tf_op jit(solution)/shard_map/all_gather | solution.py:16
  37.4 13.8 %psum.7 = f32[128]{0:T(128)S(1)} all-reduce(f32[128]{0:T(128)S(1)} %reduce_sum.57), channel_id=1, replica_groups=mesh['ep'=4,'grp'=8] {'grp'}, use_global_device_ids=true, to_apply=%region_7.8 | all-reduce | flops 128 | bytes 1024 | tf_op jit(solution)/shard_map/psum | solution.py:17
  51.2 0.0 copy-done.3
  51.2 0.5 multiply_subtract_fusion
  51.7 0.0 all-to-all-done.1
  51.7 0.1 convert_reduce_fusion
  51.8 2.8 %convolution_convert_fusion = bf16[128,4096]{1,0:T(8,128)(2,1)} fusion(f32[16,128]{1,0:T(8,128)S(1)} %get-tuple-element.3, f32[16,4096]{1,0:T(8,128)S(1)} %convert_reduce_fusion), kind=kOutput, calls=%fused_computation | convolution fusion | flops 101187584 | bytes 1318912 | tf_op jit(solution)/shard_map/dot_general | solution.py:55
  (4 shorter events, 0.1 us)
Async XLA Ops:
  0.6 19.6 %copy-start = (bf16[320,4096]{1,0:T(8,128)(2,1)S(1)}, bf16[320,4096]{1,0:T(8,128)(2,1)}, u32[]{:S(2)}) copy-start(bf16[320,4096]{1,0:T(8,128)(2,1)} %param.12) | copy-start | bytes 7864324
  2.7 16.6 %copy-start.1 = (bf16[4096,320]{0,1:T(8,128)(2,1)S(1)}, bf16[4096,320]{0,1:T(8,128)(2,1)}, u32[]{:S(2)}) copy-start(bf16[4096,320]{0,1:T(8,128)(2,1)} %param.10) | copy-start | bytes 7864324
  20.2 8.2 %copy-start.2 = (s32[128,8]{0,1:T(8,128)S(1)}, s32[128,8]{0,1:T(8,128)}, u32[]{:S(2)}) copy-start(s32[128,8]{0,1:T(8,128)} %param.8) | copy-start | bytes 12292
  20.3 30.9 %copy-start.3 = (f32[128]{0:T(128)S(1)}, f32[128]{0:T(128)}, u32[]{:S(2)}) copy-start(f32[128]{0:T(128)} %param.13) | copy-start | bytes 1540
  25.0 26.7 %all-to-all-start.1 = ((bf16[4,16,4096]{2,1,0:T(8,128)(2,1)}), bf16[4,16,4096]{2,1,0:T(8,128)(2,1)S(1)}, u32[]{:S(2)}, u32[]{:S(2)}) async-start(bf16[4,16,4096]{2,1,0:T(8,128)(2,1)} %bitcast.19), calls=%async_computation.1 | async-start | bytes 1048576 | tf_op jit(solution)/shard_map/all_to_all | solution.py:48
